TPU v7x, 512 devices: a whole 4x4x16 slice. The times are simulated.
512 devices in a mesh: grp: 4 (over x), dom: 128 (over z, y, core).
Axes of the slice: x: 4, y: 4, z: 16, core: 2. Of those that a mesh axis runs over, the one named last changes fastest.
Arguments:
- node_state: float32 [65536, 6, 128], P(('grp', 'dom')), may hold values from -6 to 6
- node_dest: int32 [65536], P(('grp', 'dom')), may hold values from 0 to 127, as said below
- seg_nodes: float32 [6, 262144], P(None, ('grp', 'dom')), may hold values from -6 to 6
- seg_conn: int32 [3, 524288], P(None, ('grp', 'dom')), may hold values from 0 to 511
- pair_seg: int32 [512, 4, 32], P(('grp', 'dom')), may hold values from 0 to 7
- pair_slot: int32 [512, 4, 32], P(('grp', 'dom')), may hold values from 0 to 255, as said below
Outputs:
- node_force: float32 [65536, 3, 128], P(('grp', 'dom'))
Inputs may be any that keep to these rules, and one draw needn't show every extreme that they name: `node_dest`: at most 2 blocks of one device name the same contact domain; in every grp row one contact domain receives exactly 2 blocks from every device of that row; every device sends at least one block to the contact domain of its own dom index. `pair_slot`: every entry names a slot d * 2 + k that holds a block: device (r, d) sends more than k blocks to the contact domain.
All inputs are finite; a program needn't handle non-finite values.
Results may differ from a plain program's by a relative error of at most 0.00023.
Values sent between devices are 32-bit elements; how exact they have to be, the bound alone decides.
A program may use at most 64 MiB of HBM per device.

v0:
```python
import math

import jax
import jax.numpy as jnp
from jax import lax
from jax.experimental import pallas as pl
from jax.experimental.pallas import tpu as pltpu
from jax.sharding import Mesh
from jax.sharding import PartitionSpec as P

AXES = ("grp", "dom_0", "dom_1", "dom_2")
NX, NZ, NY, NC = 4, 16, 4, 2
MESH = pl.DeviceIdType.MESH
PARENT = (0, 1, 0, 3, 4, 3, 6, 6)
USED = 58
BATCH = 16
ROOM = 16 << 20
F32, BF16, I32 = jnp.float32, jnp.bfloat16, jnp.int32

time_step = 0.5
stiffness = 0.5
radius_sq = 0.5
root = math.sqrt(math.log2(math.e) / radius_sq)

TURNS = sorted(
    ((a, b, c) for a in range(NX) for b in range(NY) for c in range(NC) if a or b or c),
    key=lambda t: -min(t[0], NX - t[0]) - min(t[1], NY - t[1]),
)


def start(src, dst, ss, rs, dev):
    copy = pltpu.make_async_remote_copy(
        src_ref=src, dst_ref=dst, send_sem=ss, recv_sem=rs, device_id=dev, device_id_type=MESH
    )
    copy.start()
    return copy


def landed(dst, ss, rs, dev):
    pltpu.make_async_remote_copy(
        src_ref=dst, dst_ref=dst, send_sem=ss, recv_sem=rs, device_id=dev, device_id_type=MESH
    ).wait_recv()


def geometry(seg_nodes, conn, pseg, pslot, geo):
    corners = []
    for k in range(3):
        idx = jnp.concatenate([conn[k : k + 1, b * 128 : (b + 1) * 128] for b in range(8)], axis=0)
        hi = lax.shift_right_logical(idx, 7)
        lo = lax.bitwise_and(idx, 127)
        comps = []
        for i in range(6):
            got = None
            for q in range(4):
                table = jnp.broadcast_to(seg_nodes[i : i + 1, q * 128 : (q + 1) * 128], (8, 128))
                part = jnp.take_along_axis(table, lo, axis=1)
                got = part if got is None else jnp.where(hi == q, part, got)
            comps.append(got)
        corners.append(comps)
    a, b, c = corners
    e1 = [b[i] - a[i] for i in range(3)]
    e2 = [c[i] - a[i] for i in range(3)]
    n = [0.5 * (e1[(i + 1) % 3] * e2[(i + 2) % 3] - e1[(i + 2) % 3] * e2[(i + 1) % 3]) for i in range(3)]
    m = [(a[i] + b[i] + c[i]) / 3.0 for i in range(3)]
    u = [(a[i + 3] + b[i + 3] + c[i + 3]) / 3.0 for i in range(3)]
    off = sum(n[i] * (m[i] + time_step * u[i]) for i in range(3))
    values = [2.0 * root * v for v in m] + [-stiffness * v for v in n] + [stiffness * off]
    for i, v in enumerate(values):
        geo[8 * i : 8 * i + 8, :] = v
    tables = []
    for tab in (pseg, pslot):
        t = jnp.concatenate([tab[0].astype(F32), jnp.zeros((4, 96), F32)], axis=1)
        rows = [pltpu.roll(jnp.broadcast_to(t[r : r + 1], (8, 128)), 32 * r, 1) for r in range(4)]
        tables.append(rows[0] + rows[1] + rows[2] + rows[3])
    for i, t in enumerate(tables):
        geo[56 + i : 57 + i, :] = t[0:1]


def slots_of(dest, inverse, tgt):
    i0 = lax.broadcasted_iota(I32, (128, 128), 0)
    i1 = lax.broadcasted_iota(I32, (128, 128), 1)
    wide = jnp.broadcast_to(dest[0:1, :].astype(F32), (128, 128))
    same = (wide == wide.T) & (i0 < i1)
    rank = jnp.sum(jnp.where(same, 1.0, 0.0), axis=0, keepdims=True).astype(I32)
    d = dest[0:1, :]
    z = lax.shift_right_logical(d, 3)
    p = lax.bitwise_and(z, 3) * 8 + lax.bitwise_and(d, 7)
    slot = lax.shift_right_logical(z, 2) * 2 + rank
    tgt[...] = jnp.broadcast_to(p * 24 + slot, (8, 128))
    column = jnp.broadcast_to((p * 8 + slot).astype(F32), (128, 128)).T.astype(I32)
    for half in range(2):
        found = jnp.sum(jnp.where(column == i1 + 128 * half, i0, 0).astype(F32), axis=0, keepdims=True)
        inverse[8 * half : 8 * half + 8, :] = jnp.broadcast_to(found, (8, 128)).astype(I32)


def exchange_kernel(
    dest_h, node_h, seg_h, conn_h, pseg_h, pslot_h,
    n_out, g_out, tgt,
    dest, node, seg_nodes, conn, pseg, pslot, geo, s, xb, inv_v, inv, ins, ys, yr, zs, zr, ws, wr,
):
    g, z = lax.axis_index("grp"), lax.axis_index("dom_0")
    y, c = lax.axis_index("dom_1"), lax.axis_index("dom_2")
    loads = []
    for i, (src, dst) in enumerate(
        ((conn_h, conn), (seg_h, seg_nodes), (pseg_h, pseg), (pslot_h, pslot), (dest_h, dest), (node_h, node))
    ):
        load = pltpu.make_async_copy(src, dst, ins.at[i])
        load.start()
        loads.append(load)

    def zat(k):
        return (z + k + NZ) % NZ

    quad = z % 4
    other = (quad, z - quad + g, y, c)
    diagonal = quad == g
    peers = [((g + a) % NX, z, (y + b) % NY, (c + e) % NC) for a, b, e in TURNS]
    for e in sorted({d - p for d, p in enumerate(PARENT, 1)}):
        peers += [(g, zat(e), y, c), (g, zat(-e), y, c)]
    barrier = pltpu.get_barrier_semaphore()
    for peer in peers:
        pl.semaphore_signal(barrier, inc=1, device_id=peer, device_id_type=MESH)

    @pl.when(jnp.logical_not(diagonal))
    def _():
        pl.semaphore_signal(barrier, inc=1, device_id=other, device_id_type=MESH)

    for load in loads[:4]:
        load.wait()
    geometry(seg_nodes, conn, pseg, pslot, geo)
    loads[4].wait()
    slots_of(dest, inv_v, tgt)
    table = pltpu.make_async_copy(inv_v, inv, ins.at[6])
    table.start()
    pl.semaphore_wait(barrier, len(peers) + jnp.where(diagonal, 0, 1))
    me = g * 8 + y * 2 + c

    def number(sign, d):
        return (d if sign > 0 else 8 + d) - 1

    most = {1: 8, -1: 7}

    def children(p, sign):
        mine = [d for d in range(1, most[sign] + 1) if PARENT[d - 1] == p]
        return sorted(mine, key=lambda d: (d not in PARENT, -d))

    used = pl.ds(0, USED)

    def forward_z(sign, p, src):
        for d in children(p, sign):
            k = number(sign, d)
            start(src, g_out.at[zat(-sign * p), used], zs.at[k], zr.at[k], (g, zat(sign * (d - p)), y, c))

    def arrive_z(sign, d):
        k = number(sign, d)
        slot = g_out.at[zat(-sign * d), used]
        landed(slot, zs.at[k], zr.at[k], (g, zat(-sign * (d - PARENT[d - 1])), y, c))
        forward_z(sign, d, slot)

    def node_send(k):
        a, b, e = TURNS[k]
        dev = ((g + a) % NX, z, (y + b) % NY, (c + e) % NC)
        start(s.at[dev[0] * 8 + dev[2] * 2 + dev[3]], n_out.at[me], ys.at[k], yr.at[k], dev)

    @pl.when(jnp.logical_not(diagonal))
    def _():
        start(geo.at[used], g_out.at[other[1], used], ws, wr, other)

    @pl.when(diagonal)
    def _():
        forward_z(1, 0, geo.at[used])
        forward_z(-1, 0, geo.at[used])
        g_out[z] = geo[...]

    loads[5].wait()

    def turn(j, _):
        at = pl.multiple_of(8 * j, 8)
        for i in range(3):
            x = node[pl.ds(i * 128 + at, 8), :]
            xb[pl.ds(at, 8), i, :] = x * root
            xb[pl.ds(at, 8), i + 3, :] = x + time_step * node[pl.ds((i + 3) * 128 + at, 8), :]
        return 0

    lax.fori_loop(0, 16, turn, 0, unroll=2)
    table.wait()

    def place(p, _):
        for k in range(8):
            block = xb[lax.bitwise_and(inv[8 * (p // 16), (p % 16) * 8 + k], 127)]
            s[p, pl.ds(k, 6, stride=8), :] = block[0:6]
        return 0

    lax.fori_loop(0, 32, place, 0, unroll=2)
    n_out[me] = s[me]
    first = 31
    for k in range(first):
        node_send(k)

    @pl.when(jnp.logical_not(diagonal))
    def _():
        landed(g_out.at[z, used], ws, wr, other)
        forward_z(1, 0, g_out.at[z, used])
        forward_z(-1, 0, g_out.at[z, used])

    for k in range(first, len(TURNS)):
        node_send(k)

    inner = sorted(set(PARENT) - {0})
    for d in inner + [d for d in range(1, 9) if d not in inner]:
        for sign in (1, -1):
            if d <= most[sign]:
                arrive_z(sign, d)
    for k, (a, b, e) in enumerate(TURNS):
        dev = ((g - a + NX) % NX, z, (y - b + NY) % NY, (c + e) % NC)
        landed(n_out.at[dev[0] * 8 + dev[2] * 2 + dev[3]], ys.at[k], yr.at[k], dev)

    def left(src, ss, rs, dev):
        pltpu.make_async_remote_copy(
            src_ref=src, dst_ref=src, send_sem=ss, recv_sem=rs, device_id=dev, device_id_type=MESH
        ).wait_send()

    for k, (a, b, e) in enumerate(TURNS):
        dev = ((g + a) % NX, z, (y + b) % NY, (c + e) % NC)
        left(s.at[dev[0] * 8 + dev[2] * 2 + dev[3]], ys.at[k], yr.at[k], dev)
    for sign in (1, -1):
        for d in range(1, most[sign] + 1):
            k = number(sign, d)
            p = PARENT[d - 1]
            left(g_out.at[zat(-sign * p), used], zs.at[k], zr.at[k], (g, zat(sign * (d - p)), y, c))

    @pl.when(jnp.logical_not(diagonal))
    def _():
        left(geo.at[used], ws, wr, other)


def split3(t):
    a = t.astype(BF16).astype(F32)
    r = t - a
    b = r.astype(BF16).astype(F32)
    return a, b, r - b


def force_kernel(n_in, g_in, f_out, lists_v, lists, sem):
    z = lax.axis_index("dom_0")
    seg = g_in[pl.ds(56, 16, stride=64), :]
    slot = g_in[pl.ds(57, 16, stride=64), :].astype(I32)
    lane = lax.broadcasted_iota(I32, (16, 128), 1)
    sub = lax.broadcasted_iota(I32, (16, 128), 0)
    hit = lax.shift_right_logical(slot, 4) == z
    mask = jnp.where(hit, 1.0, 0.0).astype(F32)
    low4 = lax.bitwise_and(slot, 15)
    code_a = seg + (sub * 8).astype(F32)
    who = lax.shift_right_logical(lane, 5) * 8 + lax.shift_right_logical(low4, 1)
    spot8 = lax.shift_right_logical(sub, 2) * 2 + lax.bitwise_and(low4, 1)
    code_b = (who * 8 + spot8).astype(F32)
    i0 = lax.broadcasted_iota(I32, (128, 128), 0)
    i1 = lax.broadcasted_iota(I32, (128, 128), 1)
    before = jnp.where(i0 < i1, 1.0, 0.0).astype(F32)
    inner = jnp.dot(mask, before, preferred_element_type=F32)
    total = jnp.dot(mask, jnp.ones((128, 128), F32), preferred_element_type=F32)
    j0 = lax.broadcasted_iota(I32, (16, 16), 0)
    j1 = lax.broadcasted_iota(I32, (16, 16), 1)
    above = jnp.dot(jnp.where(j1 < j0, 1.0, 0.0).astype(F32), total, preferred_element_type=F32)
    pos = (inner + above).astype(I32)
    high = jnp.where(hit, lax.shift_right_logical(pos, 7), -1)
    low = lax.bitwise_and(pos, 127)
    packed = jnp.zeros((32, 128), F32)
    for i in range(16):
        at = high[i : i + 1] == sub
        left = jnp.concatenate(
            [jnp.where(at, code_a[i : i + 1], 0.0), jnp.where(at, code_b[i : i + 1], 0.0)], axis=0
        )
        spot = jnp.where(low[i : i + 1] == i0, 1.0, 0.0).astype(F32)
        packed = packed + lax.dot_general(left, spot, (((1,), (1,)), ((), ())), preferred_element_type=F32)
    count = (total[15:16] + above[15:16]).astype(I32)
    code = packed[16:32].astype(I32)
    who = lax.shift_right_logical(code, 3)
    spot8 = lax.bitwise_and(code, 7)
    tile = packed[0:16].astype(I32)
    lists_v[0:16, :] = lax.shift_right_logical(tile, 3) * 64 + lax.bitwise_and(tile, 7)
    lists_v[16:32, :] = who * 48 + spot8
    lists_v[32:48, :] = jnp.where(sub * 128 + lane < count, who * 24 + spot8, 32 * 24)
    lists_v[48:56, :] = jnp.broadcast_to(count, (8, 128))
    copy = pltpu.make_async_copy(lists_v, lists, sem)
    copy.start()
    f_out[...] = jnp.zeros_like(f_out)
    copy.wait()

    row = lax.broadcasted_iota(I32, (8, 128), 0)
    ones = jnp.ones((8, 128), F32)
    blank = jnp.zeros((48, 128), BF16)

    def node_side(at):
        t = n_in[pl.ds(at, 6, stride=8), :]
        x0, x1, x2 = t[0:1], t[1:2], t[2:3]
        q = -(x0 * x0 + x1 * x1 + x2 * x2)
        full = jnp.concatenate([t, ones[0:1], q], axis=0)
        a, b, e = split3(full)
        return jnp.concatenate([a, b, a, e, a, b], axis=0).astype(BF16)

    def seg_side(at):
        t = g_in[pl.ds(at, 8, stride=8), :]
        m0, m1, m2 = t[0:1], t[1:2], t[2:3]
        q = -0.25 * (m0 * m0 + m1 * m1 + m2 * m2)
        dist = jnp.where(row < 3, t, jnp.where(row == 6, q, jnp.where(row == 7, 1.0, 0.0)))
        clear = jnp.where((row >= 3) & (row <= 6), t, 0.0)
        sides = []
        for v in (dist, clear):
            a, b, e = split3(v)
            sides.append(jnp.concatenate([a, a, b, a, e, b], axis=0))
        a = t.astype(BF16).astype(F32)
        return sides[0], sides[1], a, t - a

    def build(p):
        out = []
        for i in range(2):
            q = p + i
            hi, lo = lax.shift_right_logical(q, 7), lax.bitwise_and(q, 127)
            out.append((lists[hi, lo], lists[16 + hi, lo], lists[32 + hi, lo]))
        na, nb = node_side(out[0][1]), node_side(out[1][1])
        rhs = jnp.concatenate(
            [jnp.concatenate([na, blank], axis=1), jnp.concatenate([blank, nb], axis=1)], axis=0
        )
        da, ca, ha, la = seg_side(out[0][0])
        db, cb, hb, lb = seg_side(out[1][0])
        dist = jnp.concatenate([da, db], axis=0).T.astype(BF16)
        clear = jnp.concatenate([ca, cb], axis=0).T.astype(BF16)
        nothing = jnp.zeros((8, 128), F32)
        left = jnp.concatenate(
            [
                jnp.concatenate([ha, ha], axis=1),
                jnp.concatenate([la, nothing], axis=1),
                jnp.concatenate([hb, hb], axis=1),
                jnp.concatenate([lb, nothing], axis=1),
            ],
            axis=0,
        ).astype(BF16)
        return dist, clear, rhs, left, out[0][2], out[1][2]

    def pressure(e, w):
        press = jnp.exp2(e) * jnp.maximum(w, 0.0)
        p_hi = press.astype(BF16)
        p_lo = (press - p_hi.astype(F32)).astype(BF16)
        return jnp.concatenate([p_hi, p_lo], axis=0)

    def batch(i, _):
        made = [build(i * BATCH + j) for j in range(0, BATCH, 2)]
        ew = [
            (jnp.dot(m[0], m[2], preferred_element_type=F32), jnp.dot(m[1], m[2], preferred_element_type=F32))
            for m in made
        ]
        ps = [pressure(e, w) for e, w in ew]
        fs = [jnp.dot(m[3], p, preferred_element_type=F32) for m, p in zip(made, ps)]
        for m, f in zip(made, fs):
            fa = -2.0 * (f[0:8, 0:128] + f[8:16, 0:128])
            fb = -2.0 * (f[16:24, 128:256] + f[24:32, 128:256])
            for at, v in ((m[4], fa[3:6]), (m[5], fb[3:6])):
                here = pl.ds(at, 3, stride=8)
                f_out[here, :] = f_out[here, :] + v
        return 0

    lax.fori_loop(0, (lists[48, 0] + BATCH - 1) // BATCH, batch, 0)


def return_kernel(f, r_out, ys, yr):
    g, z = lax.axis_index("grp"), lax.axis_index("dom_0")
    y, c = lax.axis_index("dom_1"), lax.axis_index("dom_2")
    barrier = pltpu.get_barrier_semaphore()
    for a, b, e in TURNS:
        pl.semaphore_signal(
            barrier, inc=1, device_id=((g + a) % NX, z, (y + b) % NY, (c + e) % NC), device_id_type=MESH
        )
    pl.semaphore_wait(barrier, len(TURNS))
    me = g * 8 + y * 2 + c
    sends = []
    for k, (a, b, e) in enumerate(TURNS):
        dev = ((g + a) % NX, z, (y + b) % NY, (c + e) % NC)
        sends.append(start(f.at[dev[0] * 8 + dev[2] * 2 + dev[3]], r_out.at[me], ys.at[k], yr.at[k], dev))
    r_out[me] = f[me]
    for k, (a, b, e) in enumerate(TURNS):
        dev = ((g - a + NX) % NX, z, (y - b + NY) % NY, (c + e) % NC)
        landed(r_out.at[dev[0] * 8 + dev[2] * 2 + dev[3]], ys.at[k], yr.at[k], dev)
    for copy in sends:
        copy.wait_send()


def order_kernel(tgt, r_in, out):
    def one(i, _):
        out[pl.ds(i, 3, stride=128), :] = r_in[pl.ds(tgt[0, i], 3, stride=8), :]
        return 0

    lax.fori_loop(0, 128, one, 0, unroll=8)


def vmem():
    return pl.BlockSpec(memory_space=pltpu.VMEM)


def smem():
    return pl.BlockSpec(memory_space=pltpu.SMEM)


def shape(*dims, kind=F32):
    return jax.ShapeDtypeStruct(dims, kind)


def meet(node_state, node_dest, seg_nodes, seg_conn, pair_seg, pair_slot):
    dma = pltpu.SemaphoreType.DMA
    many = len(TURNS)
    nodes = jnp.transpose(node_state, (1, 0, 2)).reshape(768, 128)
    arrays = (node_dest.reshape(1, 128), nodes, seg_nodes, seg_conn, pair_seg, pair_slot)
    return pl.pallas_call(
        exchange_kernel,
        name="exchange",
        out_shape=(shape(32, 48, 128), shape(NZ, 64, 128), shape(8, 128, kind=I32)),
        in_specs=[pl.BlockSpec(memory_space=pltpu.HBM)] * 6,
        out_specs=(vmem(), vmem(), vmem()),
        scratch_shapes=[
            pltpu.VMEM((1, 128), I32),
            pltpu.VMEM((768, 128), F32),
            pltpu.VMEM((6, 512), F32),
            pltpu.VMEM((3, 1024), I32),
            pltpu.VMEM((1, 4, 32), I32),
            pltpu.VMEM((1, 4, 32), I32),
            pltpu.VMEM((64, 128), F32),
            pltpu.VMEM((32, 48, 128), F32),
            pltpu.VMEM((128, 8, 128), F32),
            pltpu.VMEM((16, 128), I32),
            pltpu.SMEM((16, 128), I32),
            dma((7,)),
            dma((many,)),
            dma((many,)),
            dma((15,)),
            dma((15,)),
            dma,
            dma,
        ],
        compiler_params=pltpu.CompilerParams(collective_id=0, has_side_effects=True, vmem_limit_bytes=ROOM),
    )(*(pltpu.with_memory_space_constraint(v, pltpu.HBM) for v in arrays))


def give_back(forces):
    dma = pltpu.SemaphoreType.DMA
    many = len(TURNS)
    return pl.pallas_call(
        return_kernel,
        name="giveback",
        out_shape=shape(32, 24, 128),
        in_specs=[vmem()],
        out_specs=vmem(),
        scratch_shapes=[dma((many,)), dma((many,))],
        compiler_params=pltpu.CompilerParams(collective_id=1, has_side_effects=True, vmem_limit_bytes=ROOM),
    )(forces.reshape(33, 24, 128))


def shards(node_state, node_dest, seg_nodes, seg_conn, pair_seg, pair_slot):
    dma = pltpu.SemaphoreType.DMA
    many = len(TURNS)
    met, geos, tgt = meet(node_state, node_dest, seg_nodes, seg_conn, pair_seg, pair_slot)
    forces = pl.pallas_call(
        force_kernel,
        name="forces",
        out_shape=shape(33 * 24, 128),
        in_specs=[vmem()] * 2,
        out_specs=vmem(),
        scratch_shapes=[pltpu.VMEM((56, 128), I32), pltpu.SMEM((56, 128), I32), dma],
        compiler_params=pltpu.CompilerParams(vmem_limit_bytes=ROOM),
    )(met.reshape(32 * 48, 128), geos.reshape(NZ * 64, 128))
    back = give_back(forces)
    rows = pl.pallas_call(
        order_kernel,
        name="order",
        out_shape=shape(384, 128),
        in_specs=[smem(), vmem()],
        out_specs=vmem(),
        compiler_params=pltpu.CompilerParams(vmem_limit_bytes=ROOM),
    )(tgt, back.reshape(32 * 24, 128))
    return jnp.transpose(rows.reshape(3, 128, 128), (1, 0, 2))


def solution(mesh):
    split = Mesh(mesh.devices.reshape(NX, NZ, NY, NC), AXES)
    placed = (
        P(AXES, None, None),
        P(AXES),
        P(None, AXES),
        P(None, AXES),
        P(AXES, None, None),
        P(AXES, None, None),
    )
    return jax.shard_map(
        shards, mesh=split, in_specs=placed, out_specs=P(AXES, None, None), check_vma=False
    )
```

profile of v0, /device:TPU:1, one launch (start us, length us, event | category | flops | bytes accessed | tf_op | source)
XLA Modules:
  0.0 56.5 jit_solution(11356304864783348021)
XLA Ops:
  0.0 31.8 %exchange.1 = (f32[32,48,128]{2,1,0:T(8,128)S(1)}, f32[16,64,128]{2,1,0:T(8,128)S(1)}, s32[8,128]{1,0:T(8,128)S(1)}) custom-call(s32[1,128]{1,0:T(1,128)} %bitcast.16, f32[768,128]{1,0:T(8,128)} %bitcast.15, f32[6,512]{1,0:T(8,128)} %seg_h.1, s32[3,1024]{1,0:T(4,128)} %conn_h.1, s32[1,4,32]{2,1,0:T(4,128)} %pseg_h.1, s32[1,4,32]{2,1,0:T(4,128)} %pslot_h.1), custom_call_target="tpu_custom_call" | custom-call | tf_op jit(solution)/shard_map/exchange/pallas_call | solution.py:413
  31.8 7.2 %forces.1 = f32[792,128]{1,0:T(8,128)S(1)} custom-call(f32[1536,128]{1,0:T(8,128)S(1)} %bitcast.13, f32[1024,128]{1,0:T(8,128)S(1)} %bitcast.14), custom_call_target="tpu_custom_call" | custom-call | tf_op jit(solution)/shard_map/forces/pallas_call | solution.py:461
  39.0 16.0 %giveback.1 = f32[32,24,128]{2,1,0:T(8,128)S(1)} custom-call(f32[33,24,128]{2,1,0:T(8,128)S(1)} %bitcast.11), custom_call_target="tpu_custom_call" | custom-call | tf_op jit(solution)/shard_map/giveback/pallas_call | solution.py:446
  55.0 1.6 %order.1 = f32[384,128]{1,0:T(8,128)} custom-call(s32[8,128]{1,0:T(8,128)S(1)} %get-tuple-element.8.tgt, f32[768,128]{1,0:T(8,128)S(1)} %bitcast.12), custom_call_target="tpu_custom_call" | custom-call | tf_op jit(solution)/shard_map/order/pallas_call | solution.py:471
where the time goes:
time: 56.7 us; the launch traced here: 56.5 us
  Pallas kernels  56.5 us (100%)
    pallas_call x1, Pallas kernels, meet(): pl.pallas_call(exchange_kernel, name='exchange', out_shape=(shape(32, 48,...  31.8 us
    pallas_call x1, Pallas kernels, give_back(): pl.pallas_call(return_kernel, name='giveback', out_shape=shape(32, 24, 12...  16 us
    pallas_call x1, Pallas kernels, shards(): pl.pallas_call(force_kernel, name='forces', out_shape=shape(33 * 24, 128)...  7.18 us
    pallas_call x1, Pallas kernels, shards(): pl.pallas_call(order_kernel, name='order', out_shape=shape(384, 128), in_...  1.56 us

commit v1 on v0

--- a/solution.py
+++ b/solution.py
@@ -13,7 +13,7 @@
 MESH = pl.DeviceIdType.MESH
 PARENT = (0, 1, 0, 3, 4, 3, 6, 6)
 USED = 58
-BATCH = 16
+SIZES = (32, 16, 8)
 ROOM = 16 << 20
 F32, BF16, I32 = jnp.float32, jnp.bfloat16, jnp.int32
 
@@ -93,9 +93,37 @@
         inverse[8 * half : 8 * half + 8, :] = jnp.broadcast_to(found, (8, 128)).astype(I32)
 
 
+def split3(t):
+    a = t.astype(BF16).astype(F32)
+    r = t - a
+    b = r.astype(BF16).astype(F32)
+    return a, b, r - b
+
+
+def expand(chunk, out, base):
+    row = lax.broadcasted_iota(I32, (8, 128), 0)
+    nothing = jnp.zeros((16, 128), F32)
+
+    def tile(t, _):
+        v = chunk[pl.ds(t, 7, stride=8), :]
+        m0, m1, m2 = v[0:1], v[1:2], v[2:3]
+        q = -0.25 * (m0 * m0 + m1 * m1 + m2 * m2)
+        full = jnp.concatenate([v, jnp.ones((1, 128), F32)], axis=0)
+        dist = jnp.where((row < 3) | (row == 7), full, jnp.where(row == 6, q, 0.0))
+        clear = jnp.where((row >= 3) & (row <= 6), full, 0.0)
+        rows = []
+        for side in (dist, clear):
+            a, b, e = split3(side)
+            rows += [a, a, b, a, e, b, nothing]
+        out[base + t] = jnp.concatenate(rows, axis=0).T.astype(BF16)
+        return 0
+
+    lax.fori_loop(0, 8, tile, 0, unroll=4)
+
+
 def exchange_kernel(
     dest_h, node_h, seg_h, conn_h, pseg_h, pslot_h,
-    n_out, g_out, tgt,
+    n_out, g_out, tgt, ready,
     dest, node, seg_nodes, conn, pseg, pslot, geo, s, xb, inv_v, inv, ins, ys, yr, zs, zr, ws, wr,
 ):
     g, z = lax.axis_index("grp"), lax.axis_index("dom_0")
@@ -128,10 +156,6 @@
     for load in loads[:4]:
         load.wait()
     geometry(seg_nodes, conn, pseg, pslot, geo)
-    loads[4].wait()
-    slots_of(dest, inv_v, tgt)
-    table = pltpu.make_async_copy(inv_v, inv, ins.at[6])
-    table.start()
     pl.semaphore_wait(barrier, len(peers) + jnp.where(diagonal, 0, 1))
     me = g * 8 + y * 2 + c
 
@@ -156,6 +180,7 @@
         slot = g_out.at[zat(-sign * d), used]
         landed(slot, zs.at[k], zr.at[k], (g, zat(-sign * (d - PARENT[d - 1])), y, c))
         forward_z(sign, d, slot)
+        expand(g_out.at[zat(-sign * d)], ready, zat(-sign * d) * 8)
 
     def node_send(k):
         a, b, e = TURNS[k]
@@ -172,6 +197,10 @@
         forward_z(-1, 0, geo.at[used])
         g_out[z] = geo[...]
 
+    loads[4].wait()
+    slots_of(dest, inv_v, tgt)
+    table = pltpu.make_async_copy(inv_v, inv, ins.at[6])
+    table.start()
     loads[5].wait()
 
     def turn(j, _):
@@ -206,7 +235,8 @@
     for k in range(first, len(TURNS)):
         node_send(k)
 
-    inner = sorted(set(PARENT) - {0})
+    expand(g_out.at[z], ready, z * 8)
+    inner = sorted(set(PARENT) - {0}, key=lambda d: (PARENT[d - 1], -d))
     for d in inner + [d for d in range(1, 9) if d not in inner]:
         for sign in (1, -1):
             if d <= most[sign]:
@@ -234,14 +264,7 @@
         left(geo.at[used], ws, wr, other)
 
 
-def split3(t):
-    a = t.astype(BF16).astype(F32)
-    r = t - a
-    b = r.astype(BF16).astype(F32)
-    return a, b, r - b
-
-
-def force_kernel(n_in, g_in, f_out, lists_v, lists, sem):
+def force_kernel(n_in, g_in, ready, f_out, lists_v, lists, sem):
     z = lax.axis_index("dom_0")
     seg = g_in[pl.ds(56, 16, stride=64), :]
     slot = g_in[pl.ds(57, 16, stride=64), :].astype(I32)
@@ -278,7 +301,7 @@
     who = lax.shift_right_logical(code, 3)
     spot8 = lax.bitwise_and(code, 7)
     tile = packed[0:16].astype(I32)
-    lists_v[0:16, :] = lax.shift_right_logical(tile, 3) * 64 + lax.bitwise_and(tile, 7)
+    lists_v[0:16, :] = tile
     lists_v[16:32, :] = who * 48 + spot8
     lists_v[32:48, :] = jnp.where(sub * 128 + lane < count, who * 24 + spot8, 32 * 24)
     lists_v[48:56, :] = jnp.broadcast_to(count, (8, 128))
@@ -287,9 +310,9 @@
     f_out[...] = jnp.zeros_like(f_out)
     copy.wait()
 
-    row = lax.broadcasted_iota(I32, (8, 128), 0)
     ones = jnp.ones((8, 128), F32)
     blank = jnp.zeros((48, 128), BF16)
+    gap = jnp.zeros((16, 256), BF16)
 
     def node_side(at):
         t = n_in[pl.ds(at, 6, stride=8), :]
@@ -297,70 +320,74 @@
         q = -(x0 * x0 + x1 * x1 + x2 * x2)
         full = jnp.concatenate([t, ones[0:1], q], axis=0)
         a, b, e = split3(full)
-        return jnp.concatenate([a, b, a, e, a, b], axis=0).astype(BF16)
-
-    def seg_side(at):
-        t = g_in[pl.ds(at, 8, stride=8), :]
-        m0, m1, m2 = t[0:1], t[1:2], t[2:3]
-        q = -0.25 * (m0 * m0 + m1 * m1 + m2 * m2)
-        dist = jnp.where(row < 3, t, jnp.where(row == 6, q, jnp.where(row == 7, 1.0, 0.0)))
-        clear = jnp.where((row >= 3) & (row <= 6), t, 0.0)
-        sides = []
-        for v in (dist, clear):
-            a, b, e = split3(v)
-            sides.append(jnp.concatenate([a, a, b, a, e, b], axis=0))
-        a = t.astype(BF16).astype(F32)
-        return sides[0], sides[1], a, t - a
+        side = jnp.concatenate([a, b, a, e, a, b], axis=0).astype(BF16)
+        return jnp.concatenate(
+            [
+                jnp.concatenate([side, blank], axis=1),
+                gap,
+                jnp.concatenate([blank, side], axis=1),
+                gap,
+            ],
+            axis=0,
+        )
 
     def build(p):
         out = []
+        left = []
+        nothing = jnp.zeros((8, 128), F32)
         for i in range(2):
             q = p + i
             hi, lo = lax.shift_right_logical(q, 7), lax.bitwise_and(q, 127)
-            out.append((lists[hi, lo], lists[16 + hi, lo], lists[32 + hi, lo]))
-        na, nb = node_side(out[0][1]), node_side(out[1][1])
-        rhs = jnp.concatenate(
-            [jnp.concatenate([na, blank], axis=1), jnp.concatenate([blank, nb], axis=1)], axis=0
-        )
-        da, ca, ha, la = seg_side(out[0][0])
-        db, cb, hb, lb = seg_side(out[1][0])
-        dist = jnp.concatenate([da, db], axis=0).T.astype(BF16)
-        clear = jnp.concatenate([ca, cb], axis=0).T.astype(BF16)
-        nothing = jnp.zeros((8, 128), F32)
-        left = jnp.concatenate(
-            [
-                jnp.concatenate([ha, ha], axis=1),
-                jnp.concatenate([la, nothing], axis=1),
-                jnp.concatenate([hb, hb], axis=1),
-                jnp.concatenate([lb, nothing], axis=1),
-            ],
-            axis=0,
-        ).astype(BF16)
-        return dist, clear, rhs, left, out[0][2], out[1][2]
-
-    def pressure(e, w):
-        press = jnp.exp2(e) * jnp.maximum(w, 0.0)
-        p_hi = press.astype(BF16)
-        p_lo = (press - p_hi.astype(F32)).astype(BF16)
-        return jnp.concatenate([p_hi, p_lo], axis=0)
-
-    def batch(i, _):
-        made = [build(i * BATCH + j) for j in range(0, BATCH, 2)]
-        ew = [
-            (jnp.dot(m[0], m[2], preferred_element_type=F32), jnp.dot(m[1], m[2], preferred_element_type=F32))
-            for m in made
-        ]
-        ps = [pressure(e, w) for e, w in ew]
-        fs = [jnp.dot(m[3], p, preferred_element_type=F32) for m, p in zip(made, ps)]
-        for m, f in zip(made, fs):
-            fa = -2.0 * (f[0:8, 0:128] + f[8:16, 0:128])
-            fb = -2.0 * (f[16:24, 128:256] + f[24:32, 128:256])
-            for at, v in ((m[4], fa[3:6]), (m[5], fb[3:6])):
-                here = pl.ds(at, 3, stride=8)
-                f_out[here, :] = f_out[here, :] + v
-        return 0
-
-    lax.fori_loop(0, (lists[48, 0] + BATCH - 1) // BATCH, batch, 0)
+            tile = lists[hi, lo]
+            t = g_in[pl.ds(lax.shift_right_logical(tile, 3) * 64 + lax.bitwise_and(tile, 7), 7, stride=8), :]
+            t = jnp.concatenate([t, jnp.zeros((1, 128), F32)], axis=0)
+            a = t.astype(BF16).astype(F32)
+            left += [jnp.concatenate([a, a], axis=1), jnp.concatenate([t - a, nothing], axis=1)]
+            out.append((ready[tile], node_side(lists[16 + hi, lo]), lists[32 + hi, lo]))
+        return out, jnp.concatenate(left, axis=0).astype(BF16)
+
+    def pressure(ew):
+        press = jnp.exp2(ew[:, 0:128]) * jnp.maximum(ew[:, 128:256], 0.0)
+        hi = press.astype(BF16)
+        return hi, (press - hi.astype(F32)).astype(BF16)
+
+    def run(size):
+        def batch(p):
+            made = [build(p + j) for j in range(0, size, 2)]
+            ew = [
+                [jnp.dot(tile, rhs, preferred_element_type=F32) for tile, rhs, _ in pairs] for pairs, _ in made
+            ]
+            ps = []
+            for two in ew:
+                (ha, la), (hb, lb) = pressure(two[0]), pressure(two[1])
+                ps.append(
+                    jnp.concatenate(
+                        [jnp.concatenate([ha, hb], axis=1), jnp.concatenate([la, lb], axis=1)], axis=0
+                    )
+                )
+            fs = [jnp.dot(m[1], q, preferred_element_type=F32) for m, q in zip(made, ps)]
+            for (pairs, _), f in zip(made, fs):
+                fa = -2.0 * (f[0:8, 0:128] + f[8:16, 0:128])
+                fb = -2.0 * (f[16:24, 128:256] + f[24:32, 128:256])
+                for at, v in ((pairs[0][2], fa[3:6]), (pairs[1][2], fb[3:6])):
+                    here = pl.ds(at, 3, stride=8)
+                    f_out[here, :] = f_out[here, :] + v
+
+        return batch
+
+    count = lists[48, 0]
+    done = 0
+    for size in SIZES:
+        last = size == SIZES[-1]
+        turns = (count - done + (size - 1 if last else 0)) // size
+        body = run(size)
+
+        def step(i, _, body=body, size=size, done=done):
+            body(done + i * size)
+            return 0
+
+        lax.fori_loop(0, turns, step, 0)
+        done = done + turns * size
 
 
 def return_kernel(f, r_out, ys, yr):
@@ -413,9 +440,14 @@
     return pl.pallas_call(
         exchange_kernel,
         name="exchange",
-        out_shape=(shape(32, 48, 128), shape(NZ, 64, 128), shape(8, 128, kind=I32)),
+        out_shape=(
+            shape(32, 48, 128),
+            shape(NZ, 64, 128),
+            shape(8, 128, kind=I32),
+            shape(NZ * 8, 128, 128, kind=BF16),
+        ),
         in_specs=[pl.BlockSpec(memory_space=pltpu.HBM)] * 6,
-        out_specs=(vmem(), vmem(), vmem()),
+        out_specs=(vmem(), vmem(), vmem(), vmem()),
         scratch_shapes=[
             pltpu.VMEM((1, 128), I32),
             pltpu.VMEM((768, 128), F32),
@@ -457,16 +489,16 @@
 def shards(node_state, node_dest, seg_nodes, seg_conn, pair_seg, pair_slot):
     dma = pltpu.SemaphoreType.DMA
     many = len(TURNS)
-    met, geos, tgt = meet(node_state, node_dest, seg_nodes, seg_conn, pair_seg, pair_slot)
+    met, geos, tgt, ready = meet(node_state, node_dest, seg_nodes, seg_conn, pair_seg, pair_slot)
     forces = pl.pallas_call(
         force_kernel,
         name="forces",
         out_shape=shape(33 * 24, 128),
-        in_specs=[vmem()] * 2,
+        in_specs=[vmem()] * 3,
         out_specs=vmem(),
         scratch_shapes=[pltpu.VMEM((56, 128), I32), pltpu.SMEM((56, 128), I32), dma],
         compiler_params=pltpu.CompilerParams(vmem_limit_bytes=ROOM),
-    )(met.reshape(32 * 48, 128), geos.reshape(NZ * 64, 128))
+    )(met.reshape(32 * 48, 128), geos.reshape(NZ * 64, 128), ready)
     back = give_back(forces)
     rows = pl.pallas_call(
         order_kernel,

time: 56.7 us -> 56.5 us (level)
    pallas_call x1, Pallas kernels: 7.18 us -> 5.26 us  [shards(): pl.pallas_call(force_kernel, name='forces', out_shape=shape(33 * 24, 128)...]
    pallas_call x1, Pallas kernels: 16 us -> 17.7 us  [give_back(): pl.pallas_call(return_kernel, name='giveback', out_shape=shape(32, 24, 12...]
where the time goes in v1:
time: 56.5 us
  Pallas kernels  56.5 us (100%)
    pallas_call x1, Pallas kernels, meet(): pl.pallas_call(exchange_kernel, name='exchange', out_shape=(shape(32, 48,...  31.9 us
    pallas_call x1, Pallas kernels, give_back(): pl.pallas_call(return_kernel, name='giveback', out_shape=shape(32, 24, 12...  17.7 us
    pallas_call x1, Pallas kernels, shards(): pl.pallas_call(force_kernel, name='forces', out_shape=shape(33 * 24, 128)...  5.26 us
    pallas_call x1, Pallas kernels, shards(): pl.pallas_call(order_kernel, name='order', out_shape=shape(384, 128), in_...  1.56 us

profile of v1, /device:TPU:1, one launch (start us, length us, event | category | flops | bytes accessed | tf_op | source)
XLA Modules:
  0.0 56.5 jit_solution(687820920436226156)
XLA Ops:
  0.0 31.9 %exchange.1 = (f32[32,48,128]{2,1,0:T(8,128)S(1)}, f32[16,64,128]{2,1,0:T(8,128)S(1)}, s32[8,128]{1,0:T(8,128)S(1)}, bf16[128,128,128]{2,1,0:T(8,128)(2,1)S(1)}) custom-call(s32[1,128]{1,0:T(1,128)} %bitcast.16, f32[768,128]{1,0:T(8,128)} %bitcast.15, f32[6,512]{1,0:T(8,128)} %seg_h.1, s32[3,1024]{1,0:T(4,128)} %conn_h.1, s32[1,4,32]{2,1,0:T(4,128)} %pseg_h.1, ...), custom_call_target="tpu_custom_call" | custom-call | tf_op jit(solution)/shard_map/exchange/pallas_call | solution.py:440
  31.9 5.3 %forces.1 = f32[792,128]{1,0:T(8,128)S(1)} custom-call(f32[1536,128]{1,0:T(8,128)S(1)} %bitcast.13, f32[1024,128]{1,0:T(8,128)S(1)} %bitcast.14, bf16[128,128,128]{2,1,0:T(8,128)(2,1)S(1)} %get-tuple-element.12.ready), custom_call_target="tpu_custom_call" | custom-call | tf_op jit(solution)/shard_map/forces/pallas_call | solution.py:493
  37.2 17.7 %giveback.1 = f32[32,24,128]{2,1,0:T(8,128)S(1)} custom-call(f32[33,24,128]{2,1,0:T(8,128)S(1)} %bitcast.11), custom_call_target="tpu_custom_call" | custom-call | tf_op jit(solution)/shard_map/giveback/pallas_call | solution.py:478
  54.9 1.6 %order.1 = f32[384,128]{1,0:T(8,128)} custom-call(s32[8,128]{1,0:T(8,128)S(1)} %get-tuple-element.9.tgt, f32[768,128]{1,0:T(8,128)S(1)} %bitcast.12), custom_call_target="tpu_custom_call" | custom-call | tf_op jit(solution)/shard_map/order/pallas_call | solution.py:503

commit v2 on v1

--- a/solution.py
+++ b/solution.py
@@ -12,8 +12,9 @@
 NX, NZ, NY, NC = 4, 16, 4, 2
 MESH = pl.DeviceIdType.MESH
 PARENT = (0, 1, 0, 3, 4, 3, 6, 6)
+ORDER = (1, 3, 2, 4, 6, 5, 7, 8)
 USED = 58
-SIZES = (32, 16, 8)
+SIZES = (64, 32, 16, 8)
 ROOM = 16 << 20
 F32, BF16, I32 = jnp.float32, jnp.bfloat16, jnp.int32
 
@@ -118,7 +119,7 @@
         out[base + t] = jnp.concatenate(rows, axis=0).T.astype(BF16)
         return 0
 
-    lax.fori_loop(0, 8, tile, 0, unroll=4)
+    lax.fori_loop(0, 8, tile, 0, unroll=8)
 
 
 def exchange_kernel(
@@ -236,8 +237,7 @@
         node_send(k)
 
     expand(g_out.at[z], ready, z * 8)
-    inner = sorted(set(PARENT) - {0}, key=lambda d: (PARENT[d - 1], -d))
-    for d in inner + [d for d in range(1, 9) if d not in inner]:
+    for d in ORDER:
         for sign in (1, -1):
             if d <= most[sign]:
                 arrive_z(sign, d)

time: 56.5 us -> 55 us (0.973)
  Pallas kernels: 56.5 us -> 54.9 us
    pallas_call x1, Pallas kernels: 17.7 us -> 15.2 us  [give_back(): pl.pallas_call(return_kernel, name='giveback', out_shape=shape(32, 24, 12...]
    pallas_call x1, Pallas kernels: 5.26 us -> 6.18 us  [shards(): pl.pallas_call(force_kernel, name='forces', out_shape=shape(33 * 24, 128)...]
where the time goes in v2:
time: 55 us; the launch traced here: 54.9 us
  Pallas kernels  54.9 us (100%)
    pallas_call x1, Pallas kernels, meet(): pl.pallas_call(exchange_kernel, name='exchange', out_shape=(shape(32, 48,...  31.9 us
    pallas_call x1, Pallas kernels, give_back(): pl.pallas_call(return_kernel, name='giveback', out_shape=shape(32, 24, 12...  15.2 us
    pallas_call x1, Pallas kernels, shards(): pl.pallas_call(force_kernel, name='forces', out_shape=shape(33 * 24, 128)...  6.18 us
    pallas_call x1, Pallas kernels, shards(): pl.pallas_call(order_kernel, name='order', out_shape=shape(384, 128), in_...  1.56 us

profile of v2, /device:TPU:1, one launch (start us, length us, event | category | flops | bytes accessed | tf_op | source)
XLA Modules:
  0.0 54.9 jit_solution(2955692431725627573)
XLA Ops:
  0.0 31.9 %exchange.1 = (f32[32,48,128]{2,1,0:T(8,128)S(1)}, f32[16,64,128]{2,1,0:T(8,128)S(1)}, s32[8,128]{1,0:T(8,128)S(1)}, bf16[128,128,128]{2,1,0:T(8,128)(2,1)S(1)}) custom-call(s32[1,128]{1,0:T(1,128)} %bitcast.16, f32[768,128]{1,0:T(8,128)} %bitcast.15, f32[6,512]{1,0:T(8,128)} %seg_h.1, s32[3,1024]{1,0:T(4,128)} %conn_h.1, s32[1,4,32]{2,1,0:T(4,128)} %pseg_h.1, ...), custom_call_target="tpu_custom_call" | custom-call | tf_op jit(solution)/shard_map/exchange/pallas_call | solution.py:440
  32.0 6.2 %forces.1 = f32[792,128]{1,0:T(8,128)S(1)} custom-call(f32[1536,128]{1,0:T(8,128)S(1)} %bitcast.13, f32[1024,128]{1,0:T(8,128)S(1)} %bitcast.14, bf16[128,128,128]{2,1,0:T(8,128)(2,1)S(1)} %get-tuple-element.12.ready), custom_call_target="tpu_custom_call" | custom-call | tf_op jit(solution)/shard_map/forces/pallas_call | solution.py:493
  38.1 15.2 %giveback.1 = f32[32,24,128]{2,1,0:T(8,128)S(1)} custom-call(f32[33,24,128]{2,1,0:T(8,128)S(1)} %bitcast.11), custom_call_target="tpu_custom_call" | custom-call | tf_op jit(solution)/shard_map/giveback/pallas_call | solution.py:478
  53.4 1.6 %order.1 = f32[384,128]{1,0:T(8,128)} custom-call(s32[8,128]{1,0:T(8,128)S(1)} %get-tuple-element.9.tgt, f32[768,128]{1,0:T(8,128)S(1)} %bitcast.12), custom_call_target="tpu_custom_call" | custom-call | tf_op jit(solution)/shard_map/order/pallas_call | solution.py:503

commit v3 on v2

--- a/solution.py
+++ b/solution.py
@@ -87,7 +87,7 @@
     z = lax.shift_right_logical(d, 3)
     p = lax.bitwise_and(z, 3) * 8 + lax.bitwise_and(d, 7)
     slot = lax.shift_right_logical(z, 2) * 2 + rank
-    tgt[...] = jnp.broadcast_to(p * 24 + slot, (8, 128))
+    tgt[...] = p * 24 + slot
     column = jnp.broadcast_to((p * 8 + slot).astype(F32), (128, 128)).T.astype(I32)
     for half in range(2):
         found = jnp.sum(jnp.where(column == i1 + 128 * half, i0, 0).astype(F32), axis=0, keepdims=True)
@@ -223,7 +223,7 @@
 
     lax.fori_loop(0, 32, place, 0, unroll=2)
     n_out[me] = s[me]
-    first = 31
+    first = 0
     for k in range(first):
         node_send(k)
 
@@ -417,7 +417,7 @@
         out[pl.ds(i, 3, stride=128), :] = r_in[pl.ds(tgt[0, i], 3, stride=8), :]
         return 0
 
-    lax.fori_loop(0, 128, one, 0, unroll=8)
+    lax.fori_loop(0, 128, one, 0, unroll=32)
 
 
 def vmem():
@@ -443,7 +443,7 @@
         out_shape=(
             shape(32, 48, 128),
             shape(NZ, 64, 128),
-            shape(8, 128, kind=I32),
+            shape(1, 128, kind=I32),
             shape(NZ * 8, 128, 128, kind=BF16),
         ),
         in_specs=[pl.BlockSpec(memory_space=pltpu.HBM)] * 6,

time: 55 us -> 55 us (level)
    pallas_call x1, Pallas kernels: 15.2 us -> 16.3 us  [give_back(): pl.pallas_call(return_kernel, name='giveback', out_shape=shape(32, 24, 12...]
    pallas_call x1, Pallas kernels: 6.18 us -> 5.12 us  [shards(): pl.pallas_call(force_kernel, name='forces', out_shape=shape(33 * 24, 128)...]
where the time goes in v3:
time: 55 us; the launch traced here: 54.8 us
  Pallas kernels  54.8 us (100%)
    pallas_call x1, Pallas kernels, meet(): pl.pallas_call(exchange_kernel, name='exchange', out_shape=(shape(32, 48,...  31.9 us
    pallas_call x1, Pallas kernels, give_back(): pl.pallas_call(return_kernel, name='giveback', out_shape=shape(32, 24, 12...  16.3 us
    pallas_call x1, Pallas kernels, shards(): pl.pallas_call(force_kernel, name='forces', out_shape=shape(33 * 24, 128)...  5.12 us
    pallas_call x1, Pallas kernels, shards(): pl.pallas_call(order_kernel, name='order', out_shape=shape(384, 128), in_...  1.41 us

profile of v3, /device:TPU:1, one launch (start us, length us, event | category | flops | bytes accessed | tf_op | source)
XLA Modules:
  0.0 54.8 jit_solution(11323111950980486637)
XLA Ops:
  0.0 31.9 %exchange.1 = (f32[32,48,128]{2,1,0:T(8,128)S(1)}, f32[16,64,128]{2,1,0:T(8,128)S(1)}, s32[1,128]{1,0:T(1,128)S(1)}, bf16[128,128,128]{2,1,0:T(8,128)(2,1)S(1)}) custom-call(s32[1,128]{1,0:T(1,128)} %bitcast.16, f32[768,128]{1,0:T(8,128)} %bitcast.15, f32[6,512]{1,0:T(8,128)} %seg_h.1, s32[3,1024]{1,0:T(4,128)} %conn_h.1, s32[1,4,32]{2,1,0:T(4,128)} %pseg_h.1, ...), custom_call_target="tpu_custom_call" | custom-call | tf_op jit(solution)/shard_map/exchange/pallas_call | solution.py:440
  32.0 5.1 %forces.1 = f32[792,128]{1,0:T(8,128)S(1)} custom-call(f32[1536,128]{1,0:T(8,128)S(1)} %bitcast.13, f32[1024,128]{1,0:T(8,128)S(1)} %bitcast.14, bf16[128,128,128]{2,1,0:T(8,128)(2,1)S(1)} %get-tuple-element.12.ready), custom_call_target="tpu_custom_call" | custom-call | tf_op jit(solution)/shard_map/forces/pallas_call | solution.py:493
  37.1 16.3 %giveback.1 = f32[32,24,128]{2,1,0:T(8,128)S(1)} custom-call(f32[33,24,128]{2,1,0:T(8,128)S(1)} %bitcast.11), custom_call_target="tpu_custom_call" | custom-call | tf_op jit(solution)/shard_map/giveback/pallas_call | solution.py:478
  53.4 1.4 %order.1 = f32[384,128]{1,0:T(8,128)} custom-call(s32[1,128]{1,0:T(1,128)S(1)} %get-tuple-element.9.tgt, f32[768,128]{1,0:T(8,128)S(1)} %bitcast.12), custom_call_target="tpu_custom_call" | custom-call | tf_op jit(solution)/shard_map/order/pallas_call | solution.py:503

commit v4 on v3

--- a/solution.py
+++ b/solution.py
@@ -301,14 +301,22 @@
     who = lax.shift_right_logical(code, 3)
     spot8 = lax.bitwise_and(code, 7)
     tile = packed[0:16].astype(I32)
-    lists_v[0:16, :] = tile
-    lists_v[16:32, :] = who * 48 + spot8
-    lists_v[32:48, :] = jnp.where(sub * 128 + lane < count, who * 24 + spot8, 32 * 24)
-    lists_v[48:56, :] = jnp.broadcast_to(count, (8, 128))
-    copy = pltpu.make_async_copy(lists_v, lists, sem)
+    at_node = who * 48 + spot8
+    at_force = jnp.where(sub * 128 + lane < count, who * 24 + spot8, 32 * 24)
+    for i, v in enumerate((tile, at_node, at_force)):
+        lists_v[2 * i : 2 * i + 2, :] = v[0:2]
+        lists_v[8 + 16 * i : 24 + 16 * i, :] = v
+    lists_v[6:8, :] = jnp.broadcast_to(count, (2, 128))
+    copy = pltpu.make_async_copy(lists_v.at[pl.ds(0, 8)], lists.at[pl.ds(0, 8)], sem)
     copy.start()
     f_out[...] = jnp.zeros_like(f_out)
     copy.wait()
+
+    @pl.when(lists[6, 0] > 256)
+    def _():
+        rest = pltpu.make_async_copy(lists_v.at[pl.ds(8, 48)], lists.at[pl.ds(8, 48)], sem)
+        rest.start()
+        rest.wait()
 
     ones = jnp.ones((8, 128), F32)
     blank = jnp.zeros((48, 128), BF16)
@@ -338,12 +346,12 @@
         for i in range(2):
             q = p + i
             hi, lo = lax.shift_right_logical(q, 7), lax.bitwise_and(q, 127)
-            tile = lists[hi, lo]
+            tile = lists[jnp.where(hi < 2, hi, 8 + hi), lo]
             t = g_in[pl.ds(lax.shift_right_logical(tile, 3) * 64 + lax.bitwise_and(tile, 7), 7, stride=8), :]
             t = jnp.concatenate([t, jnp.zeros((1, 128), F32)], axis=0)
             a = t.astype(BF16).astype(F32)
             left += [jnp.concatenate([a, a], axis=1), jnp.concatenate([t - a, nothing], axis=1)]
-            out.append((ready[tile], node_side(lists[16 + hi, lo]), lists[32 + hi, lo]))
+            out.append((ready[tile], node_side(lists[jnp.where(hi < 2, 2 + hi, 24 + hi), lo]), lists[jnp.where(hi < 2, 4 + hi, 40 + hi), lo]))
         return out, jnp.concatenate(left, axis=0).astype(BF16)
 
     def pressure(ew):
@@ -375,7 +383,7 @@
 
         return batch
 
-    count = lists[48, 0]
+    count = lists[6, 0]
     done = 0
     for size in SIZES:
         last = size == SIZES[-1]

time: 55 us -> 53.9 us (0.980)
  Pallas kernels: 54.8 us -> 53.5 us
    pallas_call x1, Pallas kernels: 16.3 us -> 14.6 us  [give_back(): pl.pallas_call(return_kernel, name='giveback', out_shape=shape(32, 24, 12...]
where the time goes in v4:
time: 53.9 us; the launch traced here: 53.5 us
  Pallas kernels  53.5 us (99%)
    pallas_call x1, Pallas kernels, meet(): pl.pallas_call(exchange_kernel, name='exchange', out_shape=(shape(32, 48,...  31.9 us
    pallas_call x1, Pallas kernels, give_back(): pl.pallas_call(return_kernel, name='giveback', out_shape=shape(32, 24, 12...  14.6 us
    pallas_call x1, Pallas kernels, shards(): pl.pallas_call(force_kernel, name='forces', out_shape=shape(33 * 24, 128)...  5.57 us
    pallas_call x1, Pallas kernels, shards(): pl.pallas_call(order_kernel, name='order', out_shape=shape(384, 128), in_...  1.41 us

profile of v4, /device:TPU:1, one launch (start us, length us, event | category | flops | bytes accessed | tf_op | source)
XLA Modules:
  0.0 53.5 jit_solution(17344191739233411618)
XLA Ops:
  0.0 31.9 %exchange.1 = (f32[32,48,128]{2,1,0:T(8,128)S(1)}, f32[16,64,128]{2,1,0:T(8,128)S(1)}, s32[1,128]{1,0:T(1,128)S(1)}, bf16[128,128,128]{2,1,0:T(8,128)(2,1)S(1)}) custom-call(s32[1,128]{1,0:T(1,128)} %bitcast.16, f32[768,128]{1,0:T(8,128)} %bitcast.15, f32[6,512]{1,0:T(8,128)} %seg_h.1, s32[3,1024]{1,0:T(4,128)} %conn_h.1, s32[1,4,32]{2,1,0:T(4,128)} %pseg_h.1, ...), custom_call_target="tpu_custom_call" | custom-call | tf_op jit(solution)/shard_map/exchange/pallas_call | solution.py:448
  32.0 5.6 %forces.1 = f32[792,128]{1,0:T(8,128)S(1)} custom-call(f32[1536,128]{1,0:T(8,128)S(1)} %bitcast.13, f32[1024,128]{1,0:T(8,128)S(1)} %bitcast.14, bf16[128,128,128]{2,1,0:T(8,128)(2,1)S(1)} %get-tuple-element.12.ready), custom_call_target="tpu_custom_call" | custom-call | tf_op jit(solution)/shard_map/forces/pallas_call | solution.py:501
  37.5 14.6 %giveback.1 = f32[32,24,128]{2,1,0:T(8,128)S(1)} custom-call(f32[33,24,128]{2,1,0:T(8,128)S(1)} %bitcast.11), custom_call_target="tpu_custom_call" | custom-call | tf_op jit(solution)/shard_map/giveback/pallas_call | solution.py:486
  52.1 1.4 %order.1 = f32[384,128]{1,0:T(8,128)} custom-call(s32[1,128]{1,0:T(1,128)S(1)} %get-tuple-element.9.tgt, f32[768,128]{1,0:T(8,128)S(1)} %bitcast.12), custom_call_target="tpu_custom_call" | custom-call | tf_op jit(solution)/shard_map/order/pallas_call | solution.py:511
